TPU v7x, 768 devices: a whole 4x8x12 slice. The times are simulated.
768 devices in a mesh: gx: 96 (over z_lo, y, core), gy: 2 (over z_hi), gz: 4 (over x).
Axes of the slice: x: 4, y: 8, z: 12 (z_hi: 2, z_lo: 6; z = z_hi * 6 + z_lo), core: 2. Of those that a mesh axis runs over, the one named last changes fastest.
Arguments:
- adjoint_in: float32 [19, 768, 16, 512], P(None, 'gx', 'gy', 'gz'), may hold values from -16 to 16
- forward_states: float32 [2, 19, 768, 16, 512], P(None, None, 'gx', 'gy', 'gz'), may hold values from 0.01 to 0.63
- design: float32 [768, 16, 512], P('gx', 'gy', 'gz'), may hold values from 0 to 1
- solid_mask: int32 [768, 16, 512], P('gx', 'gy', 'gz'), may hold values 0 or 1
- boundary_kind: int32 [768, 16, 512], P('gx', 'gy', 'gz'), may hold values from 0 to 2, as said below
Outputs:
- adjoint_out: float32 [19, 768, 16, 512], P(None, 'gx', 'gy', 'gz')
- sensitivity: float32 [768, 16, 512], P('gx', 'gy', 'gz')
- objective: float32 [], replicated
- sens_rms: float32 [], replicated
Inputs may be any that keep to these rules, and one draw needn't show every extreme that they name: `boundary_kind`: 1 marks inlet cells, 2 outlet cells.
All inputs are finite; a program needn't handle non-finite values. No bound on the sum of `solid_mask` on one device may be relied on, other than what follows from the above.
Results may differ from a plain program's by a relative error of at most 0.0003.
Values sent between devices are 32-bit elements; how exact they have to be, the bound alone decides.
A program may use at most 32 MiB of HBM per device.

v0:
```python
import jax
import jax.numpy as jnp
import numpy as np
from jax import lax
from jax.sharding import Mesh
from jax.sharding import PartitionSpec as P

GX = ("gx_0", "gx_1", "gx_2")
GX_GY_GZ = ("gx_0", "gx_1", "gx_2", "gy", "gz")


lattice_table = np.array(
    [
        [0, 0, 0],
        [1, 0, 0],
        [-1, 0, 0],
        [0, 1, 0],
        [0, -1, 0],
        [0, 0, 1],
        [0, 0, -1],
        [1, 1, 0],
        [-1, -1, 0],
        [1, -1, 0],
        [-1, 1, 0],
        [1, 0, 1],
        [-1, 0, -1],
        [1, 0, -1],
        [-1, 0, 1],
        [0, 1, 1],
        [0, -1, -1],
        [0, 1, -1],
        [0, -1, 1],
    ],
    dtype=np.int32,
)
velocity_table = np.array(lattice_table, dtype=np.float32)
lattice_weights = np.array([1.0 / 3] + [1.0 / 18] * 6 + [1.0 / 36] * 12, dtype=np.float32)
opposite_index = [0, 2, 1, 4, 3, 6, 5, 8, 7, 10, 9, 12, 11, 14, 13, 16, 15, 18, 17]
brinkman_max = 4.0
convexity = 0.1
inflow_speed = 0.08


def shifted(block, axis, distance):
    devices = range(lax.axis_size(axis))
    route = [(i - distance, i) for i in devices if i - distance in devices]
    return lax.ppermute(block, axis, route)


def over_axes(array, axes):
    for axis in axes:
        array = lax.psum(array, axis)
    return array


def build_relax(lattice):
    cx = lattice[:, 0].astype(np.float32)
    cy = lattice[:, 1].astype(np.float32)
    cz = lattice[:, 2].astype(np.float32)
    csq = cx * cx + cy * cy + cz * cz
    rows = [
        np.ones(19, dtype=np.float32),
        19 * csq - 30,
        (21 * csq * csq - 53 * csq + 24) / 2,
        cx,
        (5 * csq - 9) * cx,
        cy,
        (5 * csq - 9) * cy,
        cz,
        (5 * csq - 9) * cz,
        3 * cx * cx - csq,
        (3 * csq - 5) * (3 * cx * cx - csq),
        cy * cy - cz * cz,
        (3 * csq - 5) * (cy * cy - cz * cz),
        cx * cy,
        cy * cz,
        cx * cz,
        (cy * cy - cz * cz) * cx,
        (cz * cz - cx * cx) * cy,
        (cx * cx - cy * cy) * cz,
    ]
    moments = np.stack(rows).astype(np.float32)
    shear = 1.0 / 0.6
    rates = np.array(
        [
            0,
            1.19,
            1.4,
            0,
            1.2,
            0,
            1.2,
            0,
            1.2,
            shear,
            1.4,
            shear,
            1.4,
            shear,
            shear,
            shear,
            1.98,
            1.98,
            1.98,
        ],
        dtype=np.float32,
    )
    norms = np.sum(moments * moments, axis=1)
    scaled = moments.T * (rates / norms)[None, :]
    return (scaled @ moments).astype(np.float32)


def equilibrium(density, velocity):
    projected = jnp.tensordot(
        velocity_table, velocity, axes=(1, 0), precision=lax.Precision.HIGHEST
    )
    squared = jnp.sum(velocity * velocity, axis=0)
    return (
        lattice_weights[:, None, None, None]
        * density
        * (1.0 + 3.0 * projected + 4.5 * projected * projected - 1.5 * squared)
    )


def post_and_cost(dist, design, solid, kind, weight):
    relax_matrix = build_relax(lattice_table)
    density = jnp.sum(dist, axis=0)
    flux = jnp.tensordot(velocity_table.T, dist, axes=(1, 0), precision=lax.Precision.HIGHEST)
    damping = 1.0 / (1.0 + brinkman_max * convexity * (1.0 - design) / (convexity + design))
    velocity = flux / density * damping
    collided = dist - jnp.tensordot(
        relax_matrix,
        dist - equilibrium(density, velocity),
        axes=(1, 0),
        precision=lax.Precision.HIGHEST,
    )
    ones = jnp.ones_like(density)
    inflow = equilibrium(density, jnp.stack([inflow_speed * ones, 0.0 * ones, 0.0 * ones]))
    outflow = equilibrium(ones, velocity)
    bounced = jnp.stack([dist[k] for k in opposite_index])
    post = jnp.where(
        solid == 1, bounced, jnp.where(kind == 1, inflow, jnp.where(kind == 2, outflow, collided))
    )
    fluid = (solid == 0).astype(jnp.float32)
    cost = weight * fluid * 0.5 * density * jnp.sum(velocity * velocity, axis=0)
    return (post, cost)


def adjoint_step(dist, design, solid, kind, weight, pulled):

    def local(d, g):
        return post_and_cost(d, g, solid, kind, weight)

    outs, backward = jax.vjp(local, dist, design)
    new_adjoint, sens = backward((pulled, jnp.ones_like(outs[1])))
    return (new_adjoint, sens, jnp.sum(outs[1]))


def split_moving(pieces, column):
    upward = [i for i in range(19) if lattice_table[i, column] == 1]
    downward = [i for i in range(19) if lattice_table[i, column] == -1]
    return (
        upward,
        downward,
        jnp.stack([pieces[i] for i in upward]),
        jnp.stack([pieces[i] for i in downward]),
    )


def first_layer(stacked, dim):
    return lax.slice_in_dim(stacked, 0, 1, 1, dim)


def last_layer(stacked, dim):
    length = stacked.shape[dim]
    return lax.slice_in_dim(stacked, length - 1, length, 1, dim)


def place_moving(pieces, upward, downward, up_stack, down_stack, from_above, from_below, dim):
    length = up_stack.shape[dim]
    up_new = jnp.concatenate([lax.slice_in_dim(up_stack, 1, length, 1, dim), from_above], axis=dim)
    down_new = jnp.concatenate(
        [from_below, lax.slice_in_dim(down_stack, 0, length - 1, 1, dim)], axis=dim
    )
    for k, i in enumerate(upward):
        pieces[i] = up_new[k]
    for k, i in enumerate(downward):
        pieces[i] = down_new[k]
    return pieces


def pull_directed(adjoint):
    pieces = [adjoint[i] for i in range(19)]
    upward, downward, up_stack, down_stack = split_moving(pieces, 0)
    from_above = shifted(first_layer(up_stack, 1), GX, -1)
    from_below = shifted(last_layer(down_stack, 1), GX, 1)
    pieces = place_moving(pieces, upward, downward, up_stack, down_stack, from_above, from_below, 1)
    upward, downward, up_stack, down_stack = split_moving(pieces, 1)
    from_above = shifted(first_layer(up_stack, 2), "gy", -1)
    from_below = shifted(last_layer(down_stack, 2), "gy", 1)
    pieces = place_moving(pieces, upward, downward, up_stack, down_stack, from_above, from_below, 2)
    upward, downward, up_stack, down_stack = split_moving(pieces, 2)
    from_above = shifted(first_layer(up_stack, 3), "gz", -1)
    from_below = shifted(last_layer(down_stack, 3), "gz", 1)
    pieces = place_moving(pieces, upward, downward, up_stack, down_stack, from_above, from_below, 3)
    return jnp.stack(pieces)


def body(adjoint_in, forward_states, design, solid_mask, boundary_kind):
    block_x, block_y, block_z = design.shape
    whole_x = lax.axis_size(GX) * block_x
    cells = whole_x * lax.axis_size("gy") * block_y * lax.axis_size("gz") * block_z
    xpos = (lax.axis_index(GX) * block_x + jnp.arange(block_x, dtype=jnp.int32)).astype(jnp.float32)
    weight = (1.0 + 2.0 * xpos / (whole_x - 1))[:, None, None]
    adjoint = adjoint_in
    sens_total = jnp.zeros(design.shape, jnp.float32)
    cost_local = jnp.zeros((), jnp.float32)
    for t in (1, 0):
        pulled = pull_directed(adjoint)
        adjoint, sens_step, cost_step = adjoint_step(
            forward_states[t], design, solid_mask, boundary_kind, weight, pulled
        )
        sens_total = sens_total + sens_step
        cost_local = cost_local + cost_step
    cost_total, square_total = (
        over_axes(cost_local, GX_GY_GZ),
        over_axes(jnp.sum(sens_total * sens_total), GX_GY_GZ),
    )
    objective = cost_total / cells
    sens_rms = jnp.sqrt(square_total / cells + 1e-06)
    return (adjoint, sens_total / sens_rms, objective, sens_rms)


def solution(mesh):
    torus = Mesh(
        mesh.devices.reshape(6, 8, 2, mesh.shape["gy"], mesh.shape["gz"]),
        ("gx_0", "gx_1", "gx_2", "gy", "gz"),
    )
    placed = (
        P(None, GX, "gy", "gz"),
        P(None, None, GX, "gy", "gz"),
        P(GX, "gy", "gz"),
        P(GX, "gy", "gz"),
        P(GX, "gy", "gz"),
    )
    return jax.shard_map(
        body,
        mesh=torus,
        in_specs=placed,
        out_specs=(P(None, GX, "gy", "gz"), P(GX, "gy", "gz"), P(), P()),
        check_vma=False,
    )
```

profile of v0, /device:TPU:1, one launch (start us, length us, event | category | flops | bytes accessed | tf_op | source)
XLA Modules:
  0.0 183.7 jit_solution(15800848701589842359)
XLA Ops:
  0.6 1.8 fusion.116
  3.3 4.6 %collective-permute-start.1 = (f32[5,1,8,128]{3,0,2,1:T(8,128)}, f32[5,1,8,128]{3,0,2,1:T(8,128)}, u32[]{:S(2)}, u32[]{:S(2)}) collective-permute-start(f32[5,1,8,128]{3,0,2,1:T(8,128)} %slice.484), channel_id=1, source_target_pairs={{0,8},{8,16},{16,24},{24,32},{32,40},{40,48},{48,56},{56,64},{64,7... | collective-permute-start | bytes 61448 | tf_op jit(solution)/shard_map/ppermute | solution.py:47
  8.7 9.7 %collective-permute-start = (f32[5,1,8,128]{3,0,2,1:T(8,128)}, f32[5,1,8,128]{3,0,2,1:T(8,128)}, u32[]{:S(2)}, u32[]{:S(2)}) collective-permute-start(f32[5,1,8,128]{3,0,2,1:T(8,128)} %slice.483), channel_id=1, source_target_pairs={{8,0},{16,8},{24,16},{32,24},{40,32},{48,40},{56,48},{64,56},{72,6... | collective-permute-start | bytes 61448 | tf_op jit(solution)/shard_map/ppermute | solution.py:47
  25.2 7.1 %collective-permute-start.3 = (f32[5,8,1,128]{3,0,2,1:T(8,128)S(1)}, f32[5,8,1,128]{3,0,2,1:T(8,128)S(1)}, u32[]{:S(2)}, u32[]{:S(2)}) collective-permute-start(f32[5,8,1,128]{3,0,2,1:T(8,128)S(1)} %slice.488), channel_id=1, source_target_pairs={{0,4},{1,5},{2,6},{3,7},{8,12},{9,13},{10,14},{11,15},{16,20},{17,... | collective-permute-start | bytes 61448 | tf_op jit(solution)/shard_map/ppermute | solution.py:47
  34.1 9.9 %collective-permute-done.2 = f32[5,8,1,128]{3,0,2,1:T(8,128)S(1)} collective-permute-done((f32[5,8,1,128]{3,0,2,1:T(8,128)S(1)}, f32[5,8,1,128]{3,0,2,1:T(8,128)S(1)}, u32[]{:S(2)}, u32[]{:S(2)}) %collective-permute-start.2) | collective-permute-done | bytes 20512 | tf_op jit(solution)/shard_map/ppermute | solution.py:47
  44.5 3.1 %collective-permute-start.5 = (f32[5,8,8,1]{3,0,2,1:T(8,128)S(1)}, f32[5,8,8,1]{3,0,2,1:T(8,128)S(1)}, u32[]{:S(2)}, u32[]{:S(2)}) collective-permute-start(f32[5,8,8,1]{3,0,2,1:T(8,128)S(1)} %slice.492), channel_id=1, source_target_pairs={{0,1},{1,2},{2,3},{4,5},{5,6},{6,7},{8,9},{9,10},{10,11},{12,13},{... | collective-permute-start | bytes 3848 | tf_op jit(solution)/shard_map/ppermute | solution.py:47
  49.6 4.0 %collective-permute-done.5 = f32[5,8,8,1]{3,0,2,1:T(8,128)S(1)} collective-permute-done((f32[5,8,8,1]{3,0,2,1:T(8,128)S(1)}, f32[5,8,8,1]{3,0,2,1:T(8,128)S(1)}, u32[]{:S(2)}, u32[]{:S(2)}) %collective-permute-start.5) | collective-permute-done | bytes 1312 | tf_op jit(solution)/shard_map/ppermute | solution.py:47
  53.9 3.9 %collective-permute-done.4 = f32[5,8,8,1]{3,0,2,1:T(8,128)S(1)} collective-permute-done((f32[5,8,8,1]{3,0,2,1:T(8,128)S(1)}, f32[5,8,8,1]{3,0,2,1:T(8,128)S(1)}, u32[]{:S(2)}, u32[]{:S(2)}) %collective-permute-start.4) | collective-permute-done | bytes 1312 | tf_op jit(solution)/shard_map/ppermute | solution.py:47
  59.0 2.8 %multiply_reduce_fusion.1 = (f32[8,8,128]{2,1,0:T(8,128)S(1)}, f32[8,8,128]{2,1,0:T(8,128)S(1)}, f32[8,8,128]{2,1,0:T(8,128)S(1)}, f32[8,8,128]{2,1,0:T(8,128)S(...) fusion(f32[19,8,8,128]{3,0,2,1:T(8,128)} %constant.174, f32[19,8,8,128]{3,0,2,1:T(8,128)S(1)} %stack.50, ...), kind=kOutput, calls=%fused_computation.51 | convolution fusion | flops 39657472 | bytes 3335664 | tf_op jit(solution)/shard_map/transpose(jvp())/dot_general | solution.py:131
  65.7 2.2 %fusion.1 = f32[19,8,8,128]{3,0,2,1:T(8,128)S(1)} fusion(f32[3,19,1,1]{1,0,3,2:T(4,128)S(1)} %copy-done.18, f32[19,8,8,128]{3,0,2,1:T(8,128)S(1)} %get-tuple-element.177, f32[1,8,8,128]{3,0,2,1:T(1,128)S(1)} %get-tuple-element.86, f32[1,8,8,128]{3,0,2,1:T(1,128)S(1)} %get-tuple-element.87, f32[1,8,8,128]{3,0,2,1:T(1,128)S(1)} %get-tuple-element.88, ...), kind=kOutput, calls=%fused_computation.3 | convolution fusion | flops 9854976 | bytes 2679031 | tf_op jit(solution)/shard_map/transpose(jvp())/dot_general | solution.py:128
  68.7 3.6 %collective-permute-start.7 = (f32[5,1,8,128]{3,0,2,1:T(8,128)S(1)}, f32[5,1,8,128]{3,0,2,1:T(8,128)S(1)}, u32[]{:S(2)}, u32[]{:S(2)}) collective-permute-start(f32[5,1,8,128]{3,0,2,1:T(8,128)S(1)} %slice.507), channel_id=1, source_target_pairs={{0,8},{8,16},{16,24},{24,32},{32,40},{40,48},{48,56},{56,64},{64,7... | collective-permute-start | bytes 61448 | tf_op jit(solution)/shard_map/ppermute | solution.py:47
  72.7 1.9 %collective-permute-start.6 = (f32[5,1,8,128]{3,0,2,1:T(8,128)S(1)}, f32[5,1,8,128]{3,0,2,1:T(8,128)S(1)}, u32[]{:S(2)}, u32[]{:S(2)}) collective-permute-start(f32[5,1,8,128]{3,0,2,1:T(8,128)S(1)} %slice.501), channel_id=1, source_target_pairs={{8,0},{16,8},{24,16},{32,24},{40,32},{48,40},{56,48},{64,56},{72,6... | collective-permute-start | bytes 61448 | tf_op jit(solution)/shard_map/ppermute | solution.py:47
  74.8 3.2 %collective-permute-done.6 = f32[5,1,8,128]{3,0,2,1:T(8,128)S(1)} collective-permute-done((f32[5,1,8,128]{3,0,2,1:T(8,128)S(1)}, f32[5,1,8,128]{3,0,2,1:T(8,128)S(1)}, u32[]{:S(2)}, u32[]{:S(2)}) %collective-permute-start.6) | collective-permute-done | bytes 20512 | tf_op jit(solution)/shard_map/ppermute | solution.py:47
  83.8 9.6 %collective-permute-done.8 = f32[5,8,1,128]{3,0,2,1:T(8,128)S(1)} collective-permute-done((f32[5,8,1,128]{3,0,2,1:T(8,128)S(1)}, f32[5,8,1,128]{3,0,2,1:T(8,128)S(1)}, u32[]{:S(2)}, u32[]{:S(2)}) %collective-permute-start.8) | collective-permute-done | bytes 20512 | tf_op jit(solution)/shard_map/ppermute | solution.py:47
  93.9 3.1 %collective-permute-start.11 = (f32[5,8,8,1]{3,0,2,1:T(8,128)S(1)}, f32[5,8,8,1]{3,0,2,1:T(8,128)S(1)}, u32[]{:S(2)}, u32[]{:S(2)}) collective-permute-start(f32[5,8,8,1]{3,0,2,1:T(8,128)S(1)} %slice.523), channel_id=1, source_target_pairs={{0,1},{1,2},{2,3},{4,5},{5,6},{6,7},{8,9},{9,10},{10,11},{12,13},{... | collective-permute-start | bytes 3848 | tf_op jit(solution)/shard_map/ppermute | solution.py:47
  99.0 4.0 %collective-permute-done.11 = f32[5,8,8,1]{3,0,2,1:T(8,128)S(1)} collective-permute-done((f32[5,8,8,1]{3,0,2,1:T(8,128)S(1)}, f32[5,8,8,1]{3,0,2,1:T(8,128)S(1)}, u32[]{:S(2)}, u32[]{:S(2)}) %collective-permute-start.11) | collective-permute-done | bytes 1312 | tf_op jit(solution)/shard_map/ppermute | solution.py:47
  103.5 3.9 %collective-permute-done.10 = f32[5,8,8,1]{3,0,2,1:T(8,128)S(1)} collective-permute-done((f32[5,8,8,1]{3,0,2,1:T(8,128)S(1)}, f32[5,8,8,1]{3,0,2,1:T(8,128)S(1)}, u32[]{:S(2)}, u32[]{:S(2)}) %collective-permute-start.10) | collective-permute-done | bytes 1312 | tf_op jit(solution)/shard_map/ppermute | solution.py:47
  108.6 2.8 %multiply_reduce_fusion = (f32[8,8,128]{2,1,0:T(8,128)S(1)}, f32[8,8,128]{2,1,0:T(8,128)S(1)}, f32[8,8,128]{2,1,0:T(8,128)S(1)}, f32[8,8,128]{2,1,0:T(8,128)S(1)...) fusion(f32[19,8,8,128]{3,0,2,1:T(8,128)} %constant.174, f32[19,8,8,128]{3,0,2,1:T(8,128)S(1)} %stack.57, ...), kind=kOutput, calls=%fused_computation.40 | convolution fusion | flops 39657472 | bytes 3335664 | tf_op jit(solution)/shard_map/transpose(jvp())/dot_general | solution.py:131
  114.7 17.5 %all-reduce.37 = (f32[]{:T(128)}, f32[]{:T(128)}) all-reduce(f32[]{:T(128)} %get-tuple-element.42, f32[]{:T(128)S(6)} %add.175), channel_id=1, replica_groups=mesh['gx_0'=6,'gx_1'=8,'gx_2'=2,'gy'=2,'gz'=4] {'gx_0'}, use_global_device_ids=true, to_apply=%region_17.18 | all-reduce | flops 2 | bytes 16 | tf_op jit(solution)/shard_map/psum | solution.py:52
  132.2 16.3 %all-reduce.36 = (f32[]{:T(128)}, f32[]{:T(128)}) all-reduce(f32[]{:T(128)} %get-tuple-element.29, f32[]{:T(128)} %get-tuple-element.30), channel_id=1, replica_groups=mesh['gx_0'=6,'gx_1'=8,'gx_2'=2,'gy'=2,'gz'=4] {'gx_1'}, use_global_device_ids=true, to_apply=%region_18.19 | all-reduce | flops 2 | bytes 16 | tf_op jit(solution)/shard_map/psum | solution.py:52
  148.5 8.9 %all-reduce.40 = (f32[]{:T(128)}, f32[]{:T(128)}) all-reduce(f32[]{:T(128)} %get-tuple-element.27, f32[]{:T(128)} %get-tuple-element.28), channel_id=1, replica_groups=mesh['gx_0'=6,'gx_1'=8,'gx_2'=2,'gy'=2,'gz'=4] {'gx_2'}, use_global_device_ids=true, to_apply=%region_19.20 | all-reduce | flops 2 | bytes 16 | tf_op jit(solution)/shard_map/psum | solution.py:52
  157.4 10.7 %all-reduce.39 = (f32[]{:T(128)}, f32[]{:T(128)}) all-reduce(f32[]{:T(128)} %get-tuple-element.35, f32[]{:T(128)} %get-tuple-element.36), channel_id=1, replica_groups=mesh['gx_0'=6,'gx_1'=8,'gx_2'=2,'gy'=2,'gz'=4] {'gy'}, use_global_device_ids=true, to_apply=%region_20.21 | all-reduce | flops 2 | bytes 16 | tf_op jit(solution)/shard_map/psum | solution.py:52
  168.1 7.5 %all-reduce.38 = (f32[]{:T(128)}, f32[]{:T(128)}) all-reduce(f32[]{:T(128)} %get-tuple-element.33, f32[]{:T(128)} %get-tuple-element.34), channel_id=1, replica_groups=mesh['gx_0'=6,'gx_1'=8,'gx_2'=2,'gy'=2,'gz'=4] {'gz'}, use_global_device_ids=true, to_apply=%region_21.22 | all-reduce | flops 2 | bytes 16 | tf_op jit(solution)/shard_map/psum | solution.py:52
  177.6 2.2 %fusion = f32[19,8,8,128]{3,0,2,1:T(8,128)S(1)} fusion(f32[3,19,1,1]{1,0,3,2:T(4,128)S(1)} %copy-done.19, f32[19,8,8,128]{3,0,2,1:T(8,128)S(1)} %copy-done.27, f32[1,8,8,128]{3,0,2,1:T(1,128)S(1)} %get-tuple-element.49, f32[1,8,8,128]{3,0,2,1:T(1,128)S(1)} %get-tuple-element.50, f32[1,8,8,128]{3,0,2,1:T(1,128)S(1)} %get-tuple-element.51, ...), kind=kOutput, calls=%fused_computation.1 | convolution fusion | flops 9854976 | bytes 2679031 | tf_op jit(solution)/shard_map/transpose(jvp())/dot_general | solution.py:128
  (145 shorter events, 32.6 us)
Async XLA Ops:
  0.6 17.8 %copy-start = (f32[2,19,8,8,128]{4,3,2,1,0:T(8,128)S(1)}, f32[2,19,8,8,128]{4,3,2,1,0:T(8,128)}, u32[]{:S(2)}) copy-start(f32[2,19,8,8,128]{4,3,2,1,0:T(8,128)} %param.22) | copy-start | bytes 3735556
  3.3 19.5 %collective-permute-start.1 = (f32[5,1,8,128]{3,0,2,1:T(8,128)}, f32[5,1,8,128]{3,0,2,1:T(8,128)}, u32[]{:S(2)}, u32[]{:S(2)}) collective-permute-start(f32[5,1,8,128]{3,0,2,1:T(8,128)} %slice.484), channel_id=1, source_target_pairs={{0,8},{8,16},{16,24},{24,32},{32,40},{40,48},{48,56},{56,64},{64,7... | collective-permute-start | bytes 61448 | tf_op jit(solution)/shard_map/ppermute | solution.py:47
  8.7 15.1 %collective-permute-start = (f32[5,1,8,128]{3,0,2,1:T(8,128)}, f32[5,1,8,128]{3,0,2,1:T(8,128)}, u32[]{:S(2)}, u32[]{:S(2)}) collective-permute-start(f32[5,1,8,128]{3,0,2,1:T(8,128)} %slice.483), channel_id=1, source_target_pairs={{8,0},{16,8},{24,16},{32,24},{40,32},{48,40},{56,48},{64,56},{72,6... | collective-permute-start | bytes 61448 | tf_op jit(solution)/shard_map/ppermute | solution.py:47
  22.7 88.8 %copy-start.13 = (pred[8,8,128]{2,1,0:T(8,128)(4,1)}, pred[8,8,128]{2,1,0:T(8,128)(4,1)S(1)}, u32[]{:S(2)}) copy-start(pred[8,8,128]{2,1,0:T(8,128)(4,1)S(1)} %get-tuple-element.172) | copy-start | bytes 24580
  22.7 88.8 %copy-start.15 = (pred[8,8,128]{2,1,0:T(8,128)(4,1)}, pred[8,8,128]{2,1,0:T(8,128)(4,1)S(1)}, u32[]{:S(2)}) copy-start(pred[8,8,128]{2,1,0:T(8,128)(4,1)S(1)} %get-tuple-element.173) | copy-start | bytes 24580
  22.7 9.7 %copy-start.3 = (f32[1,8,8,128]{3,2,1,0:T(8,128)S(1)}, f32[1,8,8,128]{3,2,1,0:T(8,128)}, u32[]{:S(2)}) copy-start(f32[1,8,8,128]{3,2,1,0:T(8,128)} %get-tuple-element.107) | copy-start | bytes 98308
  22.7 9.7 %copy-start.4 = (f32[1,8,8,128]{3,2,1,0:T(8,128)S(1)}, f32[1,8,8,128]{3,2,1,0:T(8,128)}, u32[]{:S(2)}) copy-start(f32[1,8,8,128]{3,2,1,0:T(8,128)} %get-tuple-element.108) | copy-start | bytes 98308
  22.7 9.7 %copy-start.5 = (f32[1,8,8,128]{3,2,1,0:T(8,128)S(1)}, f32[1,8,8,128]{3,2,1,0:T(8,128)}, u32[]{:S(2)}) copy-start(f32[1,8,8,128]{3,2,1,0:T(8,128)} %get-tuple-element.109) | copy-start | bytes 98308
  25.2 8.8 %collective-permute-start.3 = (f32[5,8,1,128]{3,0,2,1:T(8,128)S(1)}, f32[5,8,1,128]{3,0,2,1:T(8,128)S(1)}, u32[]{:S(2)}, u32[]{:S(2)}) collective-permute-start(f32[5,8,1,128]{3,0,2,1:T(8,128)S(1)} %slice.488), channel_id=1, source_target_pairs={{0,4},{1,5},{2,6},{3,7},{8,12},{9,13},{10,14},{11,15},{16,20},{17,... | collective-permute-start | bytes 61448 | tf_op jit(solution)/shard_map/ppermute | solution.py:47
  32.7 11.3 %collective-permute-start.2 = (f32[5,8,1,128]{3,0,2,1:T(8,128)S(1)}, f32[5,8,1,128]{3,0,2,1:T(8,128)S(1)}, u32[]{:S(2)}, u32[]{:S(2)}) collective-permute-start(f32[5,8,1,128]{3,0,2,1:T(8,128)S(1)} %slice.487), channel_id=1, source_target_pairs={{4,0},{5,1},{6,2},{7,3},{12,8},{13,9},{14,10},{15,11},{20,16},{21,... | collective-permute-start | bytes 61448 | tf_op jit(solution)/shard_map/ppermute | solution.py:47
  44.5 9.0 %collective-permute-start.5 = (f32[5,8,8,1]{3,0,2,1:T(8,128)S(1)}, f32[5,8,8,1]{3,0,2,1:T(8,128)S(1)}, u32[]{:S(2)}, u32[]{:S(2)}) collective-permute-start(f32[5,8,8,1]{3,0,2,1:T(8,128)S(1)} %slice.492), channel_id=1, source_target_pairs={{0,1},{1,2},{2,3},{4,5},{5,6},{6,7},{8,9},{9,10},{10,11},{12,13},{... | collective-permute-start | bytes 3848 | tf_op jit(solution)/shard_map/ppermute | solution.py:47
  48.1 9.7 %collective-permute-start.4 = (f32[5,8,8,1]{3,0,2,1:T(8,128)S(1)}, f32[5,8,8,1]{3,0,2,1:T(8,128)S(1)}, u32[]{:S(2)}, u32[]{:S(2)}) collective-permute-start(f32[5,8,8,1]{3,0,2,1:T(8,128)S(1)} %bitcast.56), channel_id=1, source_target_pairs={{1,0},{2,1},{3,2},{5,4},{6,5},{7,6},{9,8},{10,9},{11,10},{13,12},{... | collective-permute-start | bytes 3848 | tf_op jit(solution)/shard_map/ppermute | solution.py:47
  68.7 5.9 %collective-permute-start.7 = (f32[5,1,8,128]{3,0,2,1:T(8,128)S(1)}, f32[5,1,8,128]{3,0,2,1:T(8,128)S(1)}, u32[]{:S(2)}, u32[]{:S(2)}) collective-permute-start(f32[5,1,8,128]{3,0,2,1:T(8,128)S(1)} %slice.507), channel_id=1, source_target_pairs={{0,8},{8,16},{16,24},{24,32},{32,40},{40,48},{48,56},{56,64},{64,7... | collective-permute-start | bytes 61448 | tf_op jit(solution)/shard_map/ppermute | solution.py:47
  72.7 5.2 %collective-permute-start.6 = (f32[5,1,8,128]{3,0,2,1:T(8,128)S(1)}, f32[5,1,8,128]{3,0,2,1:T(8,128)S(1)}, u32[]{:S(2)}, u32[]{:S(2)}) collective-permute-start(f32[5,1,8,128]{3,0,2,1:T(8,128)S(1)} %slice.501), channel_id=1, source_target_pairs={{8,0},{16,8},{24,16},{32,24},{40,32},{48,40},{56,48},{64,56},{72,6... | collective-permute-start | bytes 61448 | tf_op jit(solution)/shard_map/ppermute | solution.py:47
  78.3 5.4 %collective-permute-start.9 = (f32[5,8,1,128]{3,0,2,1:T(8,128)S(1)}, f32[5,8,1,128]{3,0,2,1:T(8,128)S(1)}, u32[]{:S(2)}, u32[]{:S(2)}) collective-permute-start(f32[5,8,1,128]{3,0,2,1:T(8,128)S(1)} %slice.517), channel_id=1, source_target_pairs={{0,4},{1,5},{2,6},{3,7},{8,12},{9,13},{10,14},{11,15},{16,20},{17,... | collective-permute-start | bytes 61448 | tf_op jit(solution)/shard_map/ppermute | solution.py:47
  82.4 11.0 %collective-permute-start.8 = (f32[5,8,1,128]{3,0,2,1:T(8,128)S(1)}, f32[5,8,1,128]{3,0,2,1:T(8,128)S(1)}, u32[]{:S(2)}, u32[]{:S(2)}) collective-permute-start(f32[5,8,1,128]{3,0,2,1:T(8,128)S(1)} %slice.513), channel_id=1, source_target_pairs={{4,0},{5,1},{6,2},{7,3},{12,8},{13,9},{14,10},{15,11},{20,16},{21,... | collective-permute-start | bytes 61448 | tf_op jit(solution)/shard_map/ppermute | solution.py:47
  93.9 9.1 %collective-permute-start.11 = (f32[5,8,8,1]{3,0,2,1:T(8,128)S(1)}, f32[5,8,8,1]{3,0,2,1:T(8,128)S(1)}, u32[]{:S(2)}, u32[]{:S(2)}) collective-permute-start(f32[5,8,8,1]{3,0,2,1:T(8,128)S(1)} %slice.523), channel_id=1, source_target_pairs={{0,1},{1,2},{2,3},{4,5},{5,6},{6,7},{8,9},{9,10},{10,11},{12,13},{... | collective-permute-start | bytes 3848 | tf_op jit(solution)/shard_map/ppermute | solution.py:47
  97.5 9.8 %collective-permute-start.10 = (f32[5,8,8,1]{3,0,2,1:T(8,128)S(1)}, f32[5,8,8,1]{3,0,2,1:T(8,128)S(1)}, u32[]{:S(2)}, u32[]{:S(2)}) collective-permute-start(f32[5,8,8,1]{3,0,2,1:T(8,128)S(1)} %bitcast.57), channel_id=1, source_target_pairs={{1,0},{2,1},{3,2},{5,4},{6,5},{7,6},{9,8},{10,9},{11,10},{13,12},{... | collective-permute-start | bytes 3848 | tf_op jit(solution)/shard_map/ppermute | solution.py:47
  114.0 63.6 %copy-start.14 = (pred[8,8,128]{2,1,0:T(8,128)(4,1)S(1)}, pred[8,8,128]{2,1,0:T(8,128)(4,1)}, u32[]{:S(2)}) copy-start(pred[8,8,128]{2,1,0:T(8,128)(4,1)} %copy-done.13) | copy-start | bytes 24580
  114.0 63.6 %copy-start.16 = (pred[8,8,128]{2,1,0:T(8,128)(4,1)S(1)}, pred[8,8,128]{2,1,0:T(8,128)(4,1)}, u32[]{:S(2)}) copy-start(pred[8,8,128]{2,1,0:T(8,128)(4,1)} %copy-done.15) | copy-start | bytes 24580
  114.0 63.6 %copy-start.19 = (f32[3,19,1,1]{1,0,3,2:T(4,128)S(1)}, f32[3,19,1,1]{1,0,3,2:T(4,128)}, u32[]{:S(2)}) copy-start(f32[3,19,1,1]{1,0,3,2:T(4,128)} %constant.176) | copy-start | bytes 688
  114.0 63.6 %copy-start.23 = (pred[19]{0:T(512)(128)(4,1)S(1)}, pred[19]{0:T(512)(128)(4,1)}, u32[]{:S(2)}) copy-start(pred[19]{0:T(512)(128)(4,1)} %constant.31.clone.1) | copy-start | bytes 61
  114.0 63.6 %copy-start.27 = (f32[19,8,8,128]{3,0,2,1:T(8,128)S(1)}, f32[19,8,8,128]{3,0,2,1:T(8,128)}, u32[]{:S(2)}) copy-start(f32[19,8,8,128]{3,0,2,1:T(8,128)} %copy-done.26) | copy-start | bytes 1867780
  114.0 63.6 %copy-start.28 = (f32[3,8,8,128]{3,0,2,1:T(4,128)S(1)}, f32[3,8,8,128]{3,0,2,1:T(4,128)}, u32[]{:S(2)}) copy-start(f32[3,8,8,128]{3,0,2,1:T(4,128)} %get-tuple-element.180) | copy-start | bytes 294916
  (17 other events, 51.0 us)
where the time goes:
time: 186 us; the launch traced here: 184 us
  blocking collectives  60.9 us (33%)
  starting transfers between devices  40.3 us (22%)
  waiting for transfers between devices  38.5 us (21%)
  matrix products  18 us (10%)
  local copies, waits for them, and re-layouts  11.4 us (6%)
  other arithmetic  7.9 us (4%)
  between operations  6.58 us (4%)
    psum x5, blocking collectives, over_axes(): array = lax.psum(array, axis)  60.9 us
    ppermute x12, starting transfers between devices, shifted(): return lax.ppermute(block, axis, route)  40.3 us
    ppermute x12, waiting for transfers between devices, shifted(): return lax.ppermute(block, axis, route)  38.5 us
    dot_general x6, matrix products, equilibrium(): jnp.tensordot(velocity_table, velocity, axes=(1, 0), precision=lax.Precis...  6.21 us
    dot_general x4, matrix products, post_and_cost(): jnp.tensordot(velocity_table.T, dist, axes=(1, 0), precision=lax.Precisio...  6.19 us
    dot_general x2, matrix products, post_and_cost(): jnp.tensordot(relax_matrix, dist - equilibrium(density, velocity), axes=(...  5.63 us
  transfers between devices with their start and end apart: 12, of which 7 were waited for; matrix products, arithmetic and copies ran while one was open for 5% of the time, Pallas kernels for 0%

commit v1 on v0

v1 whole, which is shorter than its diff:
```python
import functools

import jax
import jax.numpy as jnp
import numpy as np
from jax import lax
from jax.experimental import pallas as pl
from jax.experimental.pallas import tpu as pltpu
from jax.sharding import Mesh
from jax.sharding import PartitionSpec as P

AXES = ("gx_0", "gx_1", "gx_2", "gy", "gz")
GX = AXES[:3]
MESH = pl.DeviceIdType.MESH
f32 = jnp.float32

lattice = np.array(
    [
        [0, 0, 0],
        [1, 0, 0],
        [-1, 0, 0],
        [0, 1, 0],
        [0, -1, 0],
        [0, 0, 1],
        [0, 0, -1],
        [1, 1, 0],
        [-1, -1, 0],
        [1, -1, 0],
        [-1, 1, 0],
        [1, 0, 1],
        [-1, 0, -1],
        [1, 0, -1],
        [-1, 0, 1],
        [0, 1, 1],
        [0, -1, -1],
        [0, 1, -1],
        [0, -1, 1],
    ],
    dtype=np.int32,
)
X_PLUS, X_MINUS = [1, 7, 9, 11, 13], [2, 8, 10, 12, 14]
Y_PLUS, Y_MINUS = [3, 7, 10, 15, 17], [4, 9, 8, 18, 16]
Z_PLUS, Z_MINUS = [5, 11, 14, 15, 18], [6, 12, 13, 16, 17]
MESSAGES = (
    ("xd", (-1, 0, 0)),
    ("xu", (1, 0, 0)),
    ("zd", (0, 0, -1)),
    ("zu", (0, 0, 1)),
    ("dd", (-1, 0, -1)),
    ("uu", (1, 0, 1)),
    ("du", (-1, 0, 1)),
    ("ud", (1, 0, -1)),
    ("f", (0, 1, 0)),
    ("fxd", (-1, 1, 0)),
    ("fxu", (1, 1, 0)),
    ("fzd", (0, 1, -1)),
    ("fzu", (0, 1, 1)),
)
NEAR = range(8)
FAR = range(8, 13)


def moment_scales():
    c = lattice.astype(np.float64)
    cx, cy, cz = c[:, 0], c[:, 1], c[:, 2]
    q = cx * cx + cy * cy + cz * cz
    rows = np.stack(
        [
            np.ones(19),
            19 * q - 30,
            (21 * q * q - 53 * q + 24) / 2,
            cx,
            (5 * q - 9) * cx,
            cy,
            (5 * q - 9) * cy,
            cz,
            (5 * q - 9) * cz,
            3 * cx * cx - q,
            (3 * q - 5) * (3 * cx * cx - q),
            cy * cy - cz * cz,
            (3 * q - 5) * (cy * cy - cz * cz),
            cx * cy,
            cy * cz,
            cx * cz,
            (cy * cy - cz * cz) * cx,
            (cz * cz - cx * cx) * cy,
            (cx * cx - cy * cy) * cz,
        ]
    )
    shear = 1.0 / 0.6
    rates = np.array(
        [0, 1.19, 1.4, 0, 1.2, 0, 1.2, 0, 1.2, shear, 1.4, shear, 1.4]
        + [shear] * 3
        + [1.98] * 3
    )
    return [float(v) for v in rates / np.sum(rows * rows, axis=1)]


SCALE = moment_scales()


def step_tile(q, co):
    s = {i: q[i] + q[i + 1] for i in range(1, 19, 2)}
    d = {i: q[i] - q[i + 1] for i in range(1, 19, 2)}
    exy, exz, eyz = s[7] + s[9], s[11] + s[13], s[15] + s[17]
    mxy, mxz, myz = s[7] - s[9], s[11] - s[13], s[15] - s[17]
    sax = s[1] + s[3] + s[5]
    exa = exy + exz
    sed = exa + eyz
    dxy, exy_y = d[7] + d[9], d[7] - d[9]
    dxz, exz_z = d[11] + d[13], d[11] - d[13]
    dyz, eyz_z = d[15] + d[17], d[15] - d[17]
    dx, dy, dz = dxy + dxz, exy_y + dyz, exz_z + eyz_z
    k = SCALE
    t1 = k[1] * (8.0 * sed - 11.0 * sax - 30.0 * q[0])
    t2 = k[2] * (sed - 4.0 * sax + 12.0 * q[0])
    t4 = k[4] * (dx - 4.0 * d[1])
    t6 = k[6] * (dy - 4.0 * d[3])
    t8 = k[8] * (dz - 4.0 * d[5])
    aniso = 3.0 * s[1] - sax
    edges = sed - 3.0 * eyz
    t9 = k[9] * (aniso + edges)
    t10 = k[10] * (edges - 2.0 * aniso)
    yz = s[3] - s[5]
    exyz = exy - exz
    t11 = k[11] * (yz + exyz)
    t12 = k[12] * (exyz - 2.0 * yz)
    t13, t14, t15 = k[13] * mxy, k[14] * myz, k[15] * mxz
    t16 = k[16] * (dxy - dxz)
    t17 = k[17] * (dyz - exy_y)
    t18 = k[18] * (exz_z - eyz_z)
    raw = co["raw"] != 0.0

    def pick(a, b):
        return jnp.where(raw, a, b)

    w0, w1, w2 = 1.0 / 3.0, 1.0 / 18.0, 1.0 / 36.0
    iso = (5.0 / 9.0) * t1 - (2.0 / 9.0) * t2
    yza = (1.0 / 9.0) * t10 - (2.0 / 9.0) * t9
    yzb = (2.0 / 9.0) * t11 - (1.0 / 9.0) * t12
    s0 = pick(w0 * q[0] + w1 * sax + w2 * sed, 3.0 * t2 - 11.0 * t1)
    s1x = pick(w1 * d[1] + w2 * dx, (-2.0 / 9.0) * t4)
    s1y = pick(w1 * d[3] + w2 * dy, (-2.0 / 9.0) * t6)
    s1z = pick(w1 * d[5] + w2 * dz, (-2.0 / 9.0) * t8)
    sxx = pick(w1 * s[1] + w2 * exa, iso - 2.0 * yza)
    syy = pick(w1 * s[3] + w2 * (exy + eyz), iso + yza + yzb)
    szz = pick(w1 * s[5] + w2 * (exz + eyz), iso + yza - yzb)
    sxy = pick(w2 * mxy, (1.0 / 9.0) * t13)
    syz = pick(w2 * myz, (1.0 / 9.0) * t14)
    sxz = pick(w2 * mxz, (1.0 / 9.0) * t15)
    ux, uy, uz = co["ux"], co["uy"], co["uz"]
    fx, fy, fz = co["fx"], co["fy"], co["fz"]
    vx = sxx * fx + sxy * fy + sxz * fz
    vy = sxy * fx + syy * fy + syz * fz
    vz = sxz * fx + syz * fy + szz * fz
    usq = fx * fx + fy * fy + fz * fz
    phi = (
        s0
        + 3.0 * (s1x * fx + s1y * fy + s1z * fz)
        + 4.5 * (fx * vx + fy * vy + fz * vz)
        - 1.5 * usq * s0
    )
    reff = co["reff"]
    gx = reff * (3.0 * (s1x - fx * s0) + 9.0 * vx)
    gy = reff * (3.0 * (s1y - fy * s0) + 9.0 * vy)
    gz = reff * (3.0 * (s1z - fz * s0) + 9.0 * vz)
    gu = gx * ux + gy * uy + gz * uz
    sens = co["sd"] * gu + co["sk"]
    grho = co["mphi"] * phi - gu * co["r"] + co["kc"]
    rd, hk = co["rd"], co["hk"]
    hx, hy, hz = gx * rd + hk * ux, gy * rd + hk * uy, gz * rd + hk * uz
    mi, evh, odh = co["mi"], co["evh"], co["odh"]
    out = [None] * 19
    out[0] = 2.0 * evh * q[0] - mi * (12.0 * t2 - 30.0 * t1) + grho

    def pair(i, even, odd, ch):
        e = evh * s[i] - mi * even + grho
        o = odh * d[i] - mi * odd + ch
        out[i], out[i + 1] = e + o, e - o

    axis = -11.0 * t1 - 4.0 * t2
    e9 = 2.0 * t10 - t9
    e11 = t11 - 2.0 * t12
    pair(1, axis - 2.0 * e9, -4.0 * t4, hx)
    pair(3, axis + e9 + e11, -4.0 * t6, hy)
    pair(5, axis + e9 - e11, -4.0 * t8, hz)
    edge = 8.0 * t1 + t2
    e910, e112 = t9 + t10, t11 + t12
    bxy, bxz, byz = edge + e910 + e112, edge + e910 - e112, edge - 2.0 * e910
    t4p, t4m = t4 + t16, t4 - t16
    t6m, t6p = t6 - t17, t6 + t17
    t8p, t8m = t8 + t18, t8 - t18
    pair(7, bxy + t13, t4p + t6m, hx + hy)
    pair(9, bxy - t13, t4p - t6m, hx - hy)
    pair(11, bxz + t15, t4m + t8p, hx + hz)
    pair(13, bxz - t15, t4m - t8p, hx - hz)
    pair(15, byz + t14, t6p + t8m, hy + hz)
    pair(17, byz - t14, t6p - t8m, hy - hz)
    return out, sens


SHARED = ("raw", "mi", "evh", "odh", "mphi", "hk", "sd")
PER_STEP = ("ux", "uy", "uz", "fx", "fy", "fz", "reff", "r", "rd", "kc", "sk")


def kernel(
    planes,
    adj_hbm,
    fwd_hbm,
    design_hbm,
    solid_hbm,
    kind_hbm,
    out_ref,
    sens_ref,
    sums_ref,
    av,
    a1,
    fv,
    gv,
    solv,
    kindv,
    shared,
    steps,
    xs,
    zs,
    ys,
    es,
    xr,
    zr,
    dr,
    yr,
    er,
    part,
    zsum,
    line,
    plane,
    load_sem,
    send_sem,
    recv_sem,
    line_send,
    line_recv,
    plane_send,
    plane_recv,
    back_send,
    back_recv,
):
    nz0, ny, ncore, ngy, ngz = planes
    ngx = nz0 * ny * ncore
    iz0, iy, ic = (lax.axis_index(a) for a in GX)
    igy, igz = lax.axis_index("gy"), lax.axis_index("gz")
    me = (iz0 * ny + iy) * ncore + ic
    bx, by, bz = design_hbm.shape

    def device(g, y, z):
        return (
            lax.div(g, ny * ncore),
            lax.rem(lax.div(g, ncore), ny),
            lax.rem(g, ncore),
            y,
            z,
        )

    def target(offset):
        ox, oy, oz = offset
        return device(me + ox, 1 - igy if oy else igy, igz + oz)

    def exists(offset):
        ox, _, oz = offset
        tests = []
        if ox:
            tests.append(me > 0 if ox < 0 else me < ngx - 1)
        if oz:
            tests.append(igz > 0 if oz < 0 else igz < ngz - 1)
        if not tests:
            return None
        return functools.reduce(jnp.logical_and, tests)

    def when(test, action):
        if test is None:
            action()
        else:
            pl.when(test)(action)

    def back(offset):
        return (-offset[0], offset[1], -offset[2])

    loads = [
        (adj_hbm, av),
        (fwd_hbm.at[1], fv.at[1]),
        (design_hbm, gv),
        (solid_hbm, solv),
        (kind_hbm, kindv),
        (fwd_hbm.at[0], fv.at[0]),
    ]
    loads = [
        pltpu.make_async_copy(src, dst, load_sem.at[n])
        for n, (src, dst) in enumerate(loads)
    ]
    for copy in loads:
        copy.start()

    def refs(e, n):
        name = MESSAGES[n][0]
        return {
            "xd": lambda: (xs.at[e, 0], xr.at[e, 0]),
            "xu": lambda: (xs.at[e, 1], xr.at[e, 1]),
            "zd": lambda: (zs.at[e, 0], zr.at[e, 0]),
            "zu": lambda: (zs.at[e, 1], zr.at[e, 1]),
            "dd": lambda: (xs.at[e, 0, 3], dr.at[e, 0]),
            "uu": lambda: (xs.at[e, 1, 3], dr.at[e, 1]),
            "du": lambda: (xs.at[e, 0, 4], dr.at[e, 2]),
            "ud": lambda: (xs.at[e, 1, 4], dr.at[e, 3]),
            "f": lambda: (ys.at[e], yr.at[e]),
            "fxd": lambda: (es.at[e, 0], er.at[e, 0]),
            "fxu": lambda: (es.at[e, 1], er.at[e, 1]),
            "fzd": lambda: (es.at[e, 2], er.at[e, 2]),
            "fzu": lambda: (es.at[e, 3], er.at[e, 3]),
        }[name]()

    def copy_of(e, n):
        src, dst = refs(e, n)
        return pltpu.make_async_remote_copy(
            src_ref=src,
            dst_ref=dst,
            send_sem=send_sem.at[e, n],
            recv_sem=recv_sem.at[e, n],
            device_id=target(MESSAGES[n][1]),
            device_id_type=MESH,
        )

    for e in range(2):
        for n in range(len(MESSAGES)):
            source = exists(back(MESSAGES[n][1]))
            if source is not None:
                dst = refs(e, n)[1]

                def clear(dst=dst):
                    dst[...] = jnp.zeros(dst.shape, f32)

                pl.when(jnp.logical_not(source))(clear)

    barrier = pltpu.get_barrier_semaphore()
    waits = jnp.int32(0)
    for _, offset in MESSAGES:
        test = exists(offset)

        def hello(offset=offset):
            pl.semaphore_signal(
                barrier, inc=1, device_id=target(offset), device_id_type=MESH
            )

        when(test, hello)
        waits = waits + (1 if test is None else test.astype(jnp.int32))
    nz = nz0 * ngy
    z = igy * nz0 + iz0
    nplane = ny * ncore * ngz
    cell = (iy * ncore + ic) * ngz + igz

    def at(zz, p):
        return (
            lax.rem(zz, nz0),
            lax.div(p, ncore * ngz),
            lax.rem(lax.div(p, ngz), ncore),
            lax.div(zz, nz0),
            lax.rem(p, ngz),
        )

    first = z == 0

    @pl.when(first)
    def _():
        def up(i, c):
            pl.semaphore_signal(
                barrier, inc=1, device_id=at(i, cell), device_id_type=MESH
            )
            return c

        lax.fori_loop(1, nz, up, 0)

        def across(i, c):
            peer = lax.rem(cell + i, nplane)
            pl.semaphore_signal(
                barrier, inc=1, device_id=at(0, peer), device_id_type=MESH
            )
            return c

        lax.fori_loop(1, nplane, across, 0)

    @pl.when(jnp.logical_not(first))
    def _():
        pl.semaphore_signal(barrier, inc=1, device_id=at(0, cell), device_id_type=MESH)

    waits = waits + jnp.where(first, nz - 1 + nplane - 1, 1)

    sub = lax.broadcasted_iota(jnp.int32, (by, bz), 0)
    lane = lax.broadcasted_iota(jnp.int32, (by, bz), 1)
    low = igy == 0

    def pack(e, a):
        for n, i in enumerate(X_PLUS):
            xs[e, 0, n] = a[i, 0]
        for n, i in enumerate(X_MINUS):
            xs[e, 1, n] = a[i, bx - 1]

        def faces(pops, row):
            for n, i in enumerate(pops):
                face = a[i, :, row, :]
                ys[e, n] = face
                if n == 1:
                    es[e, 0] = face[0:1]
                if n == 2:
                    es[e, 1] = face[bx - 1 : bx]
                if n in (3, 4):
                    column = face[:, 0:1] if n == 3 else face[:, bz - 1 : bz]
                    spread = jnp.where(lane == sub, column, 0.0)
                    es[e, n - 1] = jnp.sum(spread, axis=0, keepdims=True)

        pl.when(low)(lambda: faces(Y_MINUS, by - 1))
        pl.when(jnp.logical_not(low))(lambda: faces(Y_PLUS, 0))
        for side, (pops, at_lane) in enumerate(((Z_PLUS, 0), (Z_MINUS, bz - 1))):
            packed = jnp.zeros((by, bz), f32)
            for n, i in enumerate(pops):
                for x in range(bx):
                    slot = n * bx + x
                    moved = pltpu.roll(a[i, x], (slot - at_lane) % bz, 1)
                    packed = jnp.where(lane == slot, moved, packed)
            zs[e, side] = packed

    def send(e):
        for n in (*FAR, *NEAR):
            when(exists(MESSAGES[n][1]), lambda n=n: copy_of(e, n).start())

    def receive(e, numbers):
        for n in numbers:
            when(exists(back(MESSAGES[n][1])), lambda n=n: copy_of(e, n).wait_recv())

    def sent(e):
        for n in range(len(MESSAGES)):
            when(exists(MESSAGES[n][1]), lambda n=n: copy_of(e, n).wait_send())

    def precompute(t):
        cost = jnp.zeros((by, bz), f32)
        for x in range(bx):
            g = gv[x]
            fluid = solv[x] == 0
            kind = kindv[x]
            f = [fv[t, i, x] for i in range(19)]
            xpos = (me * bx + x).astype(f32)
            weight = 1.0 + 2.0 * xpos / (ngx * bx - 1)
            fl = fluid.astype(f32)
            damping = (0.1 + g) / (0.5 + 0.6 * g)
            if t == 1:
                inside = jnp.logical_and(fluid, kind == 0).astype(f32)
                put = dict(
                    raw=(kind != 0).astype(f32),
                    mi=inside,
                    evh=0.5 * (inside + 1.0 - fl),
                    odh=0.5 * (inside - 1.0 + fl),
                    mphi=jnp.logical_and(fluid, kind != 2).astype(f32),
                    hk=weight * fl * damping,
                    sd=0.44 / ((0.5 + 0.6 * g) * (0.1 + g)),
                )
                for n, name in enumerate(SHARED):
                    shared[n, x] = put[name]
            axes = []
            for axis in range(3):
                plus = sum(f[i] for i in range(19) if lattice[i, axis] == 1)
                minus = sum(f[i] for i in range(19) if lattice[i, axis] == -1)
                axes.append(plus - minus)
            rho = sum(f)
            r = 1.0 / rho
            rd = r * damping
            ux, uy, uz = (j * rd for j in axes)
            usq = ux * ux + uy * uy + uz * uz
            inlet = kind == 1
            wfu = weight * fl * usq
            reff = jnp.where(kind == 0, rho, jnp.where(kind == 2, 1.0, 0.0)) * fl
            put = dict(
                ux=ux,
                uy=uy,
                uz=uz,
                fx=jnp.where(inlet, 0.08, ux),
                fy=jnp.where(inlet, 0.0, uy),
                fz=jnp.where(inlet, 0.0, uz),
                reff=reff,
                r=r,
                rd=rd,
                kc=-0.5 * wfu,
                sk=shared[SHARED.index("sd"), x] * wfu * rho,
            )
            for n, name in enumerate(PER_STEP):
                steps[t, n, x] = put[name]
            cost = cost + 0.5 * wfu * rho
        return cost

    def pulled_far(e):
        y = [yr[e, n] for n in range(5)]
        rows = [er[e, n] for n in range(4)]
        y[1] = jnp.where(sub == bx - 1, rows[0], pltpu.roll(y[1], bx - 1, 0))
        y[2] = jnp.where(sub == 0, rows[1], pltpu.roll(y[2], 1, 0))
        columns = [
            jnp.sum(jnp.where(lane == sub, rows[n], 0.0), axis=1, keepdims=True)
            for n in (2, 3)
        ]
        y[3] = jnp.where(lane == bz - 1, columns[0], pltpu.roll(y[3], bz - 1, 1))
        y[4] = jnp.where(lane == 0, columns[1], pltpu.roll(y[4], 1, 1))
        return y

    def near(e, a, i, x):
        cx, cy, cz = (int(v) for v in lattice[i])
        xx = x + cx
        inside = 0 <= xx < bx
        if inside:
            tile = a[i, xx]
        else:
            tile = xr[e, 0, X_PLUS.index(i)] if cx > 0 else xr[e, 1, X_MINUS.index(i)]
        if cz == 0:
            return tile
        if inside:
            pops = Z_PLUS if cz > 0 else Z_MINUS
            slot = pops.index(i) * bx + xx
            halo = pltpu.roll(
                zr[e, 0 if cz > 0 else 1], ((bz - 1 if cz > 0 else 0) - slot) % bz, 1
            )
        else:
            halo = dr[e, {11: 0, 12: 1, 13: 2, 14: 3}[i]]
            halo = pltpu.roll(halo, (bz - 1) if cz > 0 else 1, 1)
        moved = pltpu.roll(tile, (bz - 1) if cz > 0 else 1, 1)
        return jnp.where(lane == (bz - 1 if cz > 0 else 0), halo, moved)

    def step(e, a, t, write):
        total = jnp.zeros((by, bz), f32)
        far = pulled_far(e)
        up = [jnp.where(low, v, 0.0) for v in far]
        down = [jnp.where(low, 0.0, v) for v in far]
        for x in range(bx):
            q = []
            for i in range(19):
                tile = near(e, a, i, x)
                cy = int(lattice[i, 1])
                if cy > 0:
                    row = up[Y_PLUS.index(i)][x : x + 1]
                    tile = jnp.where(sub == by - 1, row, pltpu.roll(tile, by - 1, 0))
                elif cy < 0:
                    row = down[Y_MINUS.index(i)][x : x + 1]
                    tile = jnp.where(sub == 0, row, pltpu.roll(tile, 1, 0))
                q.append(tile)
            co = {name: shared[n, x] for n, name in enumerate(SHARED)}
            co.update({name: steps[t, n, x] for n, name in enumerate(PER_STEP)})
            out, sens = step_tile(q, co)
            write(x, out, sens)

    loads[0].wait()
    pack(0, av)
    pl.semaphore_wait(barrier, waits)
    send(0)
    for copy in loads[1:]:
        copy.wait()
    cost = precompute(1) + precompute(0)
    receive(0, NEAR)
    receive(0, FAR)

    def write_first(x, out, sens):
        for i in range(19):
            a1[i, x] = out[i]
        sens_ref[x] = sens

    step(0, av, 1, write_first)
    pack(1, a1)
    send(1)
    receive(1, NEAR)
    receive(1, FAR)
    squares = []

    def write_second(x, out, sens):
        for i in range(19):
            out_ref[i, x] = out[i]
        both = sens_ref[x] + sens
        sens_ref[x] = both
        squares.append(both * both)

    step(1, a1, 0, write_second)
    square = functools.reduce(jnp.add, squares)
    part[0:1] = jnp.sum(square, axis=0, keepdims=True)
    part[1:2] = jnp.sum(cost, axis=0, keepdims=True)

    @pl.when(jnp.logical_not(first))
    def _():
        up = pltpu.make_async_remote_copy(
            src_ref=part,
            dst_ref=line.at[z],
            send_sem=line_send,
            recv_sem=line_recv.at[z],
            device_id=at(0, cell),
            device_id_type=MESH,
        )
        up.start()
        up.wait_send()

    @pl.when(first)
    def _():
        total = part[...]
        for i in range(1, nz):
            pltpu.make_async_remote_copy(
                src_ref=part,
                dst_ref=line.at[i],
                send_sem=line_send,
                recv_sem=line_recv.at[i],
                device_id=at(i, cell),
                device_id_type=MESH,
            ).wait_recv()
        for i in range(1, nz):
            total = total + line[i]
        zsum[...] = total
        plane[cell] = total

        def out(i, c):
            peer = lax.rem(cell + i, nplane)
            pltpu.make_async_remote_copy(
                src_ref=zsum,
                dst_ref=plane.at[cell],
                send_sem=plane_send.at[peer],
                recv_sem=plane_recv.at[cell],
                device_id=at(0, peer),
                device_id_type=MESH,
            ).start()
            return c

        lax.fori_loop(1, nplane, out, 0)

        def arrived(i, c):
            peer = lax.rem(cell + i, nplane)
            copy = pltpu.make_async_remote_copy(
                src_ref=zsum,
                dst_ref=plane.at[peer],
                send_sem=plane_send.at[peer],
                recv_sem=plane_recv.at[peer],
                device_id=at(0, peer),
                device_id_type=MESH,
            )
            copy.wait_recv()
            copy.wait_send()
            return c

        lax.fori_loop(1, nplane, arrived, 0)
        parts = [plane[i] for i in range(nplane)]
        while len(parts) > 1:
            parts = [a + b for a, b in zip(parts[::2], parts[1::2])]
        sums_ref[...] = parts[0]

        def down(i, c):
            pltpu.make_async_remote_copy(
                src_ref=sums_ref,
                dst_ref=sums_ref,
                send_sem=back_send.at[i],
                recv_sem=back_recv,
                device_id=at(i, cell),
                device_id_type=MESH,
            ).start()
            return c

        lax.fori_loop(1, nz, down, 0)

        def gone(i, c):
            pltpu.make_async_remote_copy(
                src_ref=sums_ref,
                dst_ref=sums_ref,
                send_sem=back_send.at[i],
                recv_sem=back_recv,
                device_id=at(i, cell),
                device_id_type=MESH,
            ).wait_send()
            return c

        lax.fori_loop(1, nz, gone, 0)

    @pl.when(jnp.logical_not(first))
    def _():
        pltpu.make_async_remote_copy(
            src_ref=sums_ref,
            dst_ref=sums_ref,
            send_sem=back_send.at[0],
            recv_sem=back_recv,
            device_id=at(0, cell),
            device_id_type=MESH,
        ).wait_recv()

    sent(0)
    sent(1)


def finish_kernel(cells, adj, sens, sums, adj_out, sens_out, scal_out, buf, sems):
    copy = pltpu.make_async_copy(adj, adj_out, sems.at[0])
    copy.start()
    totals = jnp.sum(sums[...], axis=1, keepdims=True)
    rms = jnp.sqrt(totals[0:1] / cells + 1e-06)
    objective = totals[1:2] / cells
    buf[...] = sens[...] / rms[None]
    copy2 = pltpu.make_async_copy(buf, sens_out, sems.at[1])
    copy2.start()
    scal_out[0:1] = jnp.broadcast_to(objective, (1, 128))
    scal_out[1:2] = jnp.broadcast_to(rms, (1, 128))
    copy.wait()
    copy2.wait()


def body(planes, adjoint_in, forward_states, design, solid_mask, boundary_kind):
    nz0, ny, ncore, ngy, ngz = planes
    bx, by, bz = design.shape
    nz, nplane = nz0 * ngy, ny * ncore * ngz
    vmem = pl.BlockSpec(memory_space=pltpu.VMEM)
    hbm = pl.BlockSpec(memory_space=pl.ANY)
    dma = pltpu.SemaphoreType.DMA
    n = len(MESSAGES)
    adj, sens, sums = pl.pallas_call(
        functools.partial(kernel, planes),
        out_shape=(
            jax.ShapeDtypeStruct(adjoint_in.shape, f32),
            jax.ShapeDtypeStruct(design.shape, f32),
            jax.ShapeDtypeStruct((2, bz), f32),
        ),
        in_specs=[hbm] * 5,
        out_specs=(vmem, vmem, vmem),
        scratch_shapes=[
            pltpu.VMEM(adjoint_in.shape, f32),
            pltpu.VMEM(adjoint_in.shape, f32),
            pltpu.VMEM(forward_states.shape, f32),
            pltpu.VMEM(design.shape, f32),
            pltpu.VMEM(design.shape, jnp.int32),
            pltpu.VMEM(design.shape, jnp.int32),
            pltpu.VMEM((len(SHARED), bx, by, bz), f32),
            pltpu.VMEM((2, len(PER_STEP), bx, by, bz), f32),
            pltpu.VMEM((2, 2, 5, by, bz), f32),
            pltpu.VMEM((2, 2, by, bz), f32),
            pltpu.VMEM((2, 5, bx, bz), f32),
            pltpu.VMEM((2, 4, 1, bz), f32),
            pltpu.VMEM((2, 2, 5, by, bz), f32),
            pltpu.VMEM((2, 2, by, bz), f32),
            pltpu.VMEM((2, 4, by, bz), f32),
            pltpu.VMEM((2, 5, bx, bz), f32),
            pltpu.VMEM((2, 4, 1, bz), f32),
            pltpu.VMEM((2, bz), f32),
            pltpu.VMEM((2, bz), f32),
            pltpu.VMEM((nz, 2, bz), f32),
            pltpu.VMEM((nplane, 2, bz), f32),
            dma((6,)),
            dma((2, n)),
            dma((2, n)),
            dma,
            dma((nz,)),
            dma((nplane,)),
            dma((nplane,)),
            dma((nz,)),
            dma,
        ],
        compiler_params=pltpu.CompilerParams(collective_id=0, has_side_effects=True),
        name="adjoint_steps",
    )(adjoint_in, forward_states, design, solid_mask, boundary_kind)
    cells = float(nz0 * ny * ncore * bx * ngy * by * ngz * bz)
    adjoint, sensitivity, scalars = pl.pallas_call(
        functools.partial(finish_kernel, cells),
        out_shape=(
            jax.ShapeDtypeStruct(adjoint_in.shape, f32),
            jax.ShapeDtypeStruct(design.shape, f32),
            jax.ShapeDtypeStruct((2, 128), f32),
        ),
        in_specs=[vmem, vmem, vmem],
        out_specs=(hbm, hbm, vmem),
        scratch_shapes=[pltpu.VMEM(design.shape, f32), dma((2,))],
        name="finish",
    )(adj, sens, sums)
    return adjoint, sensitivity, scalars[0, 0], scalars[1, 0]


def solution(mesh):
    ngy, ngz = mesh.shape["gy"], mesh.shape["gz"]
    planes = (6, 8, 2, ngy, ngz)
    torus = Mesh(mesh.devices.reshape(planes), AXES)
    placed = (
        P(None, GX, "gy", "gz"),
        P(None, None, GX, "gy", "gz"),
        P(GX, "gy", "gz"),
        P(GX, "gy", "gz"),
        P(GX, "gy", "gz"),
    )
    return jax.shard_map(
        functools.partial(body, planes),
        mesh=torus,
        in_specs=placed,
        out_specs=(P(None, GX, "gy", "gz"), P(GX, "gy", "gz"), P(), P()),
        check_vma=False,
    )
```

time: 186 us -> 56.5 us (0.30); the launches traced: 184 us -> 56.4 us
  blocking collectives: 60.9 us -> 0 us
  Pallas kernels: 0 us -> 54.5 us
  starting transfers between devices: 40.3 us -> 0 us
  waiting for transfers between devices: 38.5 us -> 0 us
  matrix products: 18 us -> 0 us
  local copies, waits for them, and re-layouts: 11.4 us -> 1.23 us
  other arithmetic: 7.9 us -> 0 us
  between operations: 6.58 us -> 0.65 us
    psum x5 -> x0, blocking collectives: 60.9 us -> none  [over_axes(): array = lax.psum(array, axis)]
    pallas_call x0 -> x2, Pallas kernels: none -> 54.5 us  [the longest x1 52 us: body(): pl.pallas_call(functools.partial(kernel, planes), out_shape=(jax.ShapeDty...]
    ppermute x12 -> x0, starting transfers between devices: 40.3 us -> none  [shifted(): return lax.ppermute(block, axis, route)]
    ppermute x12 -> x0, waiting for transfers between devices: 38.5 us -> none  [shifted(): return lax.ppermute(block, axis, route)]
    dot_general x12 -> x0, matrix products: 18 us -> none  [the longest x6 6.21 us: equilibrium(): jnp.tensordot(velocity_table, velocity, axes=(1, 0), precision=lax.Precis...]
    another operation x16 -> x0, local copies, waits for them, and re-layouts: 5.46 us -> none  [the longest x2 1.48 us: pull_directed(): return jnp.stack(pieces)]
    concatenate x12 -> x0, other arithmetic: 3.67 us -> none  [the longest x6 1.98 us: place_moving(): jnp.concatenate([lax.slice_in_dim(up_stack, 1, length, 1, dim), from_abov...]
    slice x22 -> x1, local copies, waits for them, and re-layouts: 4.25 us -> 1.23 us  [body(): return (adjoint, sensitivity, scalars[0, 0], scalars[1, 0])]
  transfers between devices with their start and end apart: 12 -> 0, of which waited for: 7 -> 0; matrix products, arithmetic and copies ran while one was open for 5% -> 0% of each run, Pallas kernels for 0% -> 0%
where the time goes in v1:
time: 56.5 us; the launch traced here: 56.4 us
  Pallas kernels  54.5 us (96%)
  local copies, waits for them, and re-layouts  1.23 us (2%)
  between operations  0.65 us (1%)
    pallas_call x1, Pallas kernels, body(): pl.pallas_call(functools.partial(kernel, planes), out_shape=(jax.ShapeDty...  52 us
    pallas_call x1, Pallas kernels, body(): pl.pallas_call(functools.partial(finish_kernel, cells), out_shape=(jax.Sh...  2.49 us
    slice x1, local copies, waits for them, and re-layouts, body(): return (adjoint, sensitivity, scalars[0, 0], scalars[1, 0])  1.23 us

profile of v1, /device:TPU:1, one launch (start us, length us, event | category | flops | bytes accessed | tf_op | source)
XLA Modules:
  0.0 56.4 jit_solution(10970234752364320167)
XLA Ops:
  0.6 52.0 %adjoint_steps.1 = (f32[19,8,8,128]{3,2,1,0:T(8,128)}, f32[8,8,128]{2,1,0:T(8,128)}, f32[2,128]{1,0:T(2,128)}) custom-call(f32[19,8,8,128]{3,2,1,0:T(8,128)} %adj_hbm.1, f32[2,19,8,8,128]{4,3,2,1,0:T(8,128)} %fwd_hbm.1, f32[8,8,128]{2,1,0:T(8,128)} %design_hbm.1, s32[8,8,128]{2,1,0:T(8,128)} %solid_hbm.1, s32[8,8,128]{2,1,0:T(8,128)} %kind_hbm.1), custom_call_target="tpu_custom_call" | custom-call | tf_op jit(solution)/shard_map/adjoint_steps/pallas_call | solution.py:715
  52.6 2.5 %finish.1 = (f32[19,8,8,128]{3,2,1,0:T(8,128)}, f32[8,8,128]{2,1,0:T(8,128)}, f32[2,128]{1,0:T(2,128)}) custom-call(f32[19,8,8,128]{3,2,1,0:T(8,128)} %get-tuple-element.10.adj, f32[8,8,128]{2,1,0:T(8,128)} %get-tuple-element.11.sens, f32[2,128]{1,0:T(2,128)} %get-tuple-element.12.sums), custom_call_target="tpu_custom_call" | custom-call | tf_op jit(solution)/shard_map/finish/pallas_call | solution.py:760
  55.1 1.2 %fusion = (f32[1,1]{1,0:T(1,128)}, f32[1,1]{1,0:T(1,128)}) fusion(f32[2,128]{1,0:T(2,128)} %get-tuple-element.15), kind=kLoop, calls=%fused_computation | loop fusion | bytes 16 | tf_op jit(solution)/shard_map/slice | solution.py:772
